TPU v7x, 512 devices: a 4x2x32 block of a 4x8x32 slice. The times are simulated.
512 devices in a mesh: rep: 2 (over y), gx: 128 (over x, z), gy: 2 (over core).
Axes of the slice: x: 4, y: 2, z: 32, core: 2. Of those that a mesh axis runs over, the one named last changes fastest.
The devices are a block of a 4x8x32 slice.
Arguments:
- tokens: bfloat16 [768, 8192], P(('rep', 'gx'), 'gy'), parts along dimension 0, may hold values from -6 to 6
- segment_ids: int32 [768], P(('rep', 'gx')), parts along dimension 0, may hold values from 0 to 1, as said below
- gate_weight: bfloat16 [8192, 2, 13312], P(None, 'gy', 'gx'), may hold values from -0.0625 to 0.0625
- up_weight: bfloat16 [8192, 2, 13312], P(None, 'gy', 'gx'), may hold values from -0.0625 to 0.0625
- down_weight: bfloat16 [2, 13312, 8192], P('gy', None, 'gx'), may hold values from -0.0390625 to 0.0390625
Outputs:
- grouped: bfloat16 [768, 8192], P(('rep', 'gx'), 'gy'), parts along dimension 0
There are 2 independent parts, one for each index of `rep`. A program takes and returns all parts, laid end to end along the dimension named above; an argument that names none is the same for every part. Nothing has to cross between parts.
Inputs may be any that keep to these rules, and one draw needn't show every extreme that they name: `segment_ids`: exactly 320 entries are 0 and 64 entries are 1.
All inputs are finite; a program needn't handle non-finite values.
Results may differ from a plain program's by a relative error of at most 0.0049.
Values may be sent and summed in bfloat16 or wider, within the bound.
No kernel may reach another device: no remote copies, remote signals or barrier semaphores. Data moves between devices by JAX's collectives and lax.ppermute only.
A program may use at most 128 MiB of HBM per device.

v0:
```python
import jax
import jax.numpy as jnp
from jax import lax
from jax.sharding import Mesh
from jax.sharding import PartitionSpec as P

PREFILL = 320
GX = ("gx_0", "gx_1")
REP_GX = ("rep", "gx_0", "gx_1")


def gather_axes(shard, axes, dim):
    for axis in reversed(axes):
        shard = lax.all_gather(shard, axis, axis=dim, tiled=True)
    return shard


def from_everyone(shard, axis):
    copies = jnp.broadcast_to(shard, (lax.axis_size(axis), *shard.shape))
    return lax.all_to_all(copies, axis, split_axis=0, concat_axis=0, tiled=True)


def laid_out(blocks, dim):
    dims = list(blocks.shape[1:])
    dims[dim] *= blocks.shape[0]
    return jnp.moveaxis(blocks, 0, dim).reshape(dims)


def gathered_copies(shard, axis, dim):
    blocks = from_everyone(shard, axis)
    return laid_out(blocks, dim)


def all_blocks(shard, axes, sequence):
    blocks = shard[None]
    for k in sequence:
        blocks = lax.all_gather(blocks, axes[k], axis=0, tiled=True)
    current = [lax.axis_size(axes[k]) for k in reversed(sequence)]
    blocks = blocks.reshape(*current, *shard.shape)
    turned = sorted(range(len(sequence)), key=lambda place: sequence[len(sequence) - 1 - place])
    return blocks.transpose(*turned, *range(len(sequence), blocks.ndim)).reshape(-1, *shard.shape)


def gather_axes_2(shard, axes, sequence, dim):
    return laid_out(all_blocks(shard, axes, sequence), dim)


def cut_along(shard, dim, count):
    before, after = (shard.shape[:dim], shard.shape[dim + 1 :])
    return jnp.moveaxis(shard.reshape(*before, count, -1, *after), dim, 0)


def summed_on_arrival(shard, axis, dim):
    count = lax.axis_size(axis)
    blocks = lax.all_to_all(cut_along(shard, dim, count), axis, 0, 0, tiled=True)
    return jnp.sum(blocks, axis=0)


def grouped_target(token_kinds):
    decode_flag = token_kinds.astype(jnp.int32)
    prefill_flag = 1 - decode_flag
    prefill_rank = jnp.cumsum(prefill_flag) - 1
    decode_rank = jnp.cumsum(decode_flag) - 1
    return jnp.where(decode_flag == 0, prefill_rank, PREFILL + decode_rank)


def local(tokens, segment_ids, gate_weight, up_weight, down_weight):
    half_rows, token_kinds = (gather_axes(tokens, GX, 0), gather_axes(segment_ids, GX, 0))
    gathered = gathered_copies(half_rows, "gy", 1)
    gate_local = gate_weight.reshape(gate_weight.shape[0], -1)
    up_local = up_weight.reshape(up_weight.shape[0], -1)
    down_local = down_weight.reshape(-1, down_weight.shape[2])
    target = grouped_target(token_kinds)
    gate_value = jnp.dot(gathered, gate_local, preferred_element_type=jnp.float32)
    up_value = jnp.dot(gathered, up_local, preferred_element_type=jnp.float32)
    hidden = (jax.nn.silu(gate_value) * up_value).astype(jnp.bfloat16)
    partial_value = jnp.dot(
        gather_axes_2(hidden, GX, (0, 1), 1), down_local, preferred_element_type=jnp.float32
    )
    placed = jnp.zeros_like(partial_value).at[target].set(partial_value)
    switched = lax.all_to_all(placed, GX, split_axis=0, concat_axis=1, tiled=True)
    return summed_on_arrival(switched, "gy", 1).astype(jnp.bfloat16)


def solution(mesh):
    torus = Mesh(
        mesh.devices.reshape(mesh.shape["rep"], 4, 32, mesh.shape["gy"]),
        ("rep", "gx_0", "gx_1", "gy"),
    )
    placed = (P(REP_GX, "gy"), P(REP_GX), P(None, "gy", GX), P(None, "gy", GX), P("gy", None, GX))
    return jax.shard_map(
        local, mesh=torus, in_specs=placed, out_specs=P(REP_GX, "gy"), check_vma=False
    )
```

profile of v0, /device:TPU:33, one launch (start us, length us, event | category | flops | bytes accessed | tf_op | source)
XLA Modules:
  0.0 413.4 jit_solution(14316246672419341581)
XLA Ops:
  6.6 88.2 %all-gather.1 = bf16[32,3,4096]{2,1,0:T(4,128)(2,1)S(1)} all-gather(bf16[1,3,4096]{2,1,0:T(4,128)(2,1)} %bitcast.53), channel_id=1, replica_groups=mesh['rep'=2,'gx_0'=4,'gx_1'=32,'gy'=2] {'gx_1'}, dimensions={0}, use_global_device_ids=true | all-gather | bytes 811008 | tf_op jit(solution)/shard_map/all_gather | solution.py:14
  94.7 1.4 reshape.89
  96.3 53.2 %all-gather.5.cloned.1.call-done = bf16[384,4096]{1,0:T(8,128)(2,1)} async-done(((bf16[96,4096]{1,0:T(8,128)(2,1)}), bf16[384,4096]{1,0:T(8,128)(2,1)}) %all-gather.5.cloned.1.call-update) | async-done | bytes 3145744 | tf_op jit(solution)/shard_map/all_gather | solution.py:14
  149.5 4.7 %copy.14 = bf16[384,4096]{0,1:T(8,128)(2,1)} copy(bf16[384,4096]{1,0:T(8,128)(2,1)} %all-gather.5.cloned.1.call-done) | data formatting | bytes 6291456 | tf_op jit(solution)/shard_map/all_gather | solution.py:14
  154.2 2.4 broadcast_in_dim.14
  156.6 9.3 %all_to_all.26 = bf16[2,384,4096]{1,2,0:T(8,128)(2,1)S(1)} all-to-all(bf16[2,384,4096]{1,2,0:T(8,128)(2,1)S(1)} %broadcast_in_dim.14), channel_id=1, replica_groups=mesh['rep'=2,'gx_0'=4,'gx_1'=32,'gy'=2] {'gy'}, dimensions={0} | all-to-all | bytes 12582912 | tf_op jit(solution)/shard_map/all_to_all | solution.py:20
  165.9 1.2 fusion.4
  167.3 1.2 fusion.9
  168.5 9.7 %all-gather = bf16[1536,104]{0,1:T(8,128)(2,1)S(1)} all-gather(bf16[384,104]{0,1:T(8,128)(2,1)S(1)} %fusion.9), channel_id=2, replica_groups=mesh['rep'=2,'gx_0'=4,'gx_1'=32,'gy'=2] {'gx_0'}, dimensions={0}, use_global_device_ids=true | all-gather | bytes 399360 | tf_op jit(solution)/shard_map/all_gather | solution.py:37
  178.2 0.7 copy.23
  179.0 1.3 dynamic-slice
  180.3 1.3 dynamic-slice.1
  183.1 33.9 %all-reduce = s32[96]{0:T(128)S(1)} all-reduce(s32[96]{0:T(128)S(1)} %dynamic-update-slice), channel_id=1, replica_groups=mesh['rep'=2,'gx_0'=4,'gx_1'=32,'gy'=2] {'gx_1'}, use_global_device_ids=true, to_apply=%add | all-reduce | flops 96 | bytes 768
  217.2 5.6 %all-reduce.1 = s32[384]{0:T(512)S(1)} all-reduce(s32[384]{0:T(512)S(1)} %dynamic-update-slice.1), channel_id=1, replica_groups=mesh['rep'=2,'gx_0'=4,'gx_1'=32,'gy'=2] {'gx_0'}, use_global_device_ids=true, to_apply=%add.1 | all-reduce | flops 384 | bytes 3072
  222.8 0.3 reduce-window.16
  223.9 96.5 %all-gather.7.cloned.1.call-done = bf16[128,384,104]{1,2,0:T(8,128)(2,1)} async-done(((bf16[4,384,104]{1,2,0:T(8,128)(2,1)}), bf16[128,384,104]{1,2,0:T(8,128)(2,1)}) %all-gather.7.cloned.1.call-update) | async-done | bytes 10223632 | tf_op jit(solution)/shard_map/all_gather | solution.py:37
  320.3 8.9 %copy.16 = bf16[4,32,384,104]{2,3,1,0:T(8,128)(2,1)} copy(bf16[4,32,384,104]{2,3,0,1:T(8,128)(2,1)} %bitcast.47) | data formatting | bytes 20447232 | tf_op jit(solution)/shard_map/transpose | solution.py:41
  329.2 6.2 %fusion = f32[384,64]{1,0:T(8,128)} fusion(bf16[384,13312]{0,1:T(8,128)(2,1)} %bitcast.48, bf16[1,13312,64]{1,2,0:T(8,128)(2,1)S(1)} %copy-done.2), kind=kOutput, calls=%fused_computation.1 | convolution fusion | flops 654311424 | bytes 12025856 | tf_op jit(solution)/shard_map/dot_general | solution.py:77
  335.4 1.9 scatter_custom_fusion
  337.6 45.1 %all_to_all.27 = f32[128,1,192]{2,1,0:T(1,128)S(1)} all-to-all(f32[128,1,192]{2,1,0:T(1,128)S(1)} %reshape.98), channel_id=1, replica_groups=mesh['rep'=2,'gx_0'=4,'gx_1'=32,'gy'=2] {'gx_0','gx_1'}, dimensions={0} | all-to-all | bytes 196608 | tf_op jit(solution)/shard_map/all_to_all | solution.py:81
  382.7 0.5 broadcast.39
  383.2 1.0 reduce.4
  384.6 21.4 %all_to_all.28 = f32[2,3,4096]{2,1,0:T(4,128)S(1)} all-to-all(f32[2,3,4096]{2,1,0:T(4,128)S(1)} %copy.19), channel_id=1, replica_groups=mesh['rep'=2,'gx_0'=4,'gx_1'=32,'gy'=2] {'gy'}, dimensions={0} | all-to-all | bytes 196608 | tf_op jit(solution)/shard_map/all_to_all | solution.py:55
  405.9 0.6 reduce_sum.9
  (30 shorter events, 2.3 us)
Async XLA Ops:
  6.5 159.3 %copy-start = (bf16[8192,1,104]{0,2,1:T(8,128)(2,1)S(1)}, bf16[8192,1,104]{0,2,1:T(8,128)(2,1)}, u32[]{:S(2)}) copy-start(bf16[8192,1,104]{0,2,1:T(8,128)(2,1)} %param.7) | copy-start | bytes 5111812
  6.6 142.9 %all-gather.5.cloned.1.call-start = ((), (), s32[]{:S(2)}) async-start(), calls=%async_computation.3 | async-start | bytes 3932160 | tf_op jit(solution)/shard_map/all_gather | solution.py:14
  96.2 224.2 %all-gather.7.cloned.1.call-start = ((), (), s32[]{:S(2)}) async-start(), calls=%async_computation.4 | async-start | bytes 10543104 | tf_op jit(solution)/shard_map/all_gather | solution.py:37
  165.9 1.5 copy-start.1
  167.3 15.6 %copy-start.3 = (s32[3]{0:T(128)S(1)}, s32[3]{0:T(128)}, u32[]{:S(2)}) copy-start(s32[3]{0:T(128)} %param.6) | copy-start | bytes 40
  320.3 8.9 %copy-start.2 = (bf16[1,13312,64]{1,2,0:T(8,128)(2,1)S(1)}, bf16[1,13312,64]{1,2,0:T(8,128)(2,1)}, u32[]{:S(2)}) copy-start(bf16[1,13312,64]{1,2,0:T(8,128)(2,1)} %param.9) | copy-start | bytes 5111812
Sparse Core Ops, SparseCore 0:
  96.3 53.1 all-gather.4
  179.1 141.1 all-gather.6
where the time goes:
time: 414 us; the launch traced here: 413 us
  blocking collectives  213 us (51%)
  waiting for transfers between devices  150 us (36%)
  local copies, waits for them, and re-layouts  24.7 us (6%)
  between operations  14.8 us (4%)
  matrix products  8.6 us (2%)
    all_gather x1, waiting for transfers between devices, all_blocks(): blocks = lax.all_gather(blocks, axes[k], axis=0, tiled=True)  96.5 us
    all_gather x1, blocking collectives, gather_axes(): shard = lax.all_gather(shard, axis, axis=dim, tiled=True)  88.2 us
    all_gather x1, waiting for transfers between devices, gather_axes(): shard = lax.all_gather(shard, axis, axis=dim, tiled=True)  53.2 us
    all_to_all x1, blocking collectives, local(): lax.all_to_all(placed, GX, split_axis=0, concat_axis=1, tiled=True)  45.1 us
    unnamed x2, blocking collectives  39.5 us
    all_to_all x1, blocking collectives, summed_on_arrival(): lax.all_to_all(cut_along(shard, dim, count), axis, 0, 0, tiled=True)  21.4 us
    all_gather x1, blocking collectives, all_blocks(): blocks = lax.all_gather(blocks, axes[k], axis=0, tiled=True)  9.68 us
    all_to_all x1, blocking collectives, from_everyone(): return lax.all_to_all(copies, axis, split_axis=0, concat_axis=0, tiled=True)  9.27 us
  transfers between devices with their start and end apart: 2, of which 2 were waited for; matrix products, arithmetic and copies ran while one was open for 1% of the time, Pallas kernels for 0%

commit v1 on v0

--- a/solution.py
+++ b/solution.py
@@ -3,6 +3,7 @@
 from jax import lax
 from jax.sharding import Mesh
 from jax.sharding import PartitionSpec as P
+from jax.lax import all_to_all, axis_size
 
 PREFILL = 320
 GX = ("gx_0", "gx_1")
@@ -34,7 +35,11 @@
 def all_blocks(shard, axes, sequence):
     blocks = shard[None]
     for k in sequence:
-        blocks = lax.all_gather(blocks, axes[k], axis=0, tiled=True)
+        mine = axes[k]
+        left_arr = axis_size(mine)
+        upper = jnp.stack([blocks] * left_arr)
+        reached = all_to_all(upper, mine, 0, 0)
+        blocks = jnp.concatenate(reached, axis=0)
     current = [lax.axis_size(axes[k]) for k in reversed(sequence)]
     blocks = blocks.reshape(*current, *shard.shape)
     turned = sorted(range(len(sequence)), key=lambda place: sequence[len(sequence) - 1 - place])

time: 414 us -> 1200 us (2.90)
  blocking collectives: 213 us -> 1070 us
  waiting for transfers between devices: 150 us -> 53.3 us
  starting transfers between devices: 0.07 us -> 23.3 us
    unnamed x2, blocking collectives: 39.5 us -> 900 us
    all_gather x1 -> x0, waiting for transfers between devices: 96.5 us -> none  [all_blocks(): blocks = lax.all_gather(blocks, axes[k], axis=0, tiled=True)]
    all_to_all x0 -> x1, starting transfers between devices: none -> 23.3 us  [all_blocks(): reached = all_to_all(upper, mine, 0, 0)]
  transfers between devices with their start and end apart: 2 -> 2, of which waited for: 2 -> 1; matrix products, arithmetic and copies ran while one was open for 1% -> 0% of each run, Pallas kernels for 0% -> 0%
where the time goes in v1:
time: 1200 us
  blocking collectives  1070 us (89%)
  waiting for transfers between devices  53.3 us (4%)
  local copies, waits for them, and re-layouts  29 us (2%)
  starting transfers between devices  23.3 us (2%)
  between operations  14.9 us (1%)
    unnamed x2, blocking collectives  900 us
    all_gather x1, blocking collectives, gather_axes(): shard = lax.all_gather(shard, axis, axis=dim, tiled=True)  88.2 us
    all_to_all x1, blocking collectives, local(): lax.all_to_all(placed, GX, split_axis=0, concat_axis=1, tiled=True)  54.5 us
    all_gather x1, waiting for transfers between devices, gather_axes(): shard = lax.all_gather(shard, axis, axis=dim, tiled=True)  53.3 us
  transfers between devices with their start and end apart: 2, of which 1 were waited for; matrix products, arithmetic and copies ran while one was open for 0% of the time, Pallas kernels for 0%

profile of v1, /device:TPU:33, one launch (start us, length us, event | category | flops | bytes accessed | tf_op | source)
XLA Modules:
  0.0 1202.8 jit_solution(11869476464979512778)
XLA Ops:
  6.6 88.2 %all-gather = bf16[32,3,4096]{2,1,0:T(4,128)(2,1)S(1)} all-gather(bf16[1,3,4096]{2,1,0:T(4,128)(2,1)} %bitcast.47), channel_id=1, replica_groups=mesh['rep'=2,'gx_0'=4,'gx_1'=32,'gy'=2] {'gx_1'}, dimensions={0}, use_global_device_ids=true | all-gather | bytes 811008 | tf_op jit(solution)/shard_map/all_gather | solution.py:15
  94.7 1.4 reshape.88
  96.2 53.3 %all-gather.3.cloned.1.call-done = bf16[384,4096]{1,0:T(8,128)(2,1)} async-done(((bf16[96,4096]{1,0:T(8,128)(2,1)}), bf16[384,4096]{1,0:T(8,128)(2,1)}) %all-gather.3.cloned.1.call-update) | async-done | bytes 3145744 | tf_op jit(solution)/shard_map/all_gather | solution.py:15
  149.5 4.7 copy.10
  154.2 2.4 broadcast_in_dim.11
  156.6 9.3 all_to_all.36
  165.9 1.2 fusion.4
  167.3 1.2 fusion.9
  168.6 9.4 all_to_all.37
  178.0 4.7 stack.7
  182.7 23.3 %all-to-all-start.2 = ((bf16[32,4,384,104]{2,3,1,0:T(8,128)(2,1)}), bf16[32,4,384,104]{2,3,1,0:T(8,128)(2,1)}, u32[]{:S(2)}, u32[]{:S(2)}) async-start(bf16[32,4,384,104]{2,3,1,0:T(8,128)(2,1)} %stack.7), calls=%async_computation.2 | async-start | bytes 20447232 | tf_op jit(solution)/shard_map/all_to_all | solution.py:41
  206.1 1.3 dynamic-slice
  207.3 1.3 dynamic-slice.1
  210.3 894.9 %all-reduce = s32[96]{0:T(128)S(1)} all-reduce(s32[96]{0:T(128)S(1)} %dynamic-update-slice), channel_id=1, replica_groups=mesh['rep'=2,'gx_0'=4,'gx_1'=32,'gy'=2] {'gx_1'}, use_global_device_ids=true, to_apply=%add | all-reduce | flops 96 | bytes 768
  1105.4 4.8 all-reduce.1
  1110.1 0.3 reduce-window.16
  1111.2 8.9 copy.11
  1120.1 6.2 fusion
  1126.3 2.0 scatter_custom_fusion
  1128.7 54.5 %all_to_all.38 = f32[128,1,192]{2,1,0:T(1,128)S(1)} all-to-all(f32[128,1,192]{2,1,0:T(1,128)S(1)} %reshape.97), channel_id=1, replica_groups=mesh['rep'=2,'gx_0'=4,'gx_1'=32,'gy'=2] {'gx_0','gx_1'}, dimensions={0} | all-to-all | bytes 196608 | tf_op jit(solution)/shard_map/all_to_all | solution.py:86
  1183.2 0.5 broadcast.42
  1183.7 1.0 reduce.4
  1185.1 10.3 all_to_all.39
  1195.3 0.6 reduce_sum.9
  (30 shorter events, 2.2 us)
Async XLA Ops:
  6.5 159.3 %copy-start = (bf16[8192,1,104]{0,2,1:T(8,128)(2,1)S(1)}, bf16[8192,1,104]{0,2,1:T(8,128)(2,1)}, u32[]{:S(2)}) copy-start(bf16[8192,1,104]{0,2,1:T(8,128)(2,1)} %param.7) | copy-start | bytes 5111812
  6.6 142.9 %all-gather.3.cloned.1.call-start = ((), (), s32[]{:S(2)}) async-start(), calls=%async_computation.5 | async-start | bytes 3932160 | tf_op jit(solution)/shard_map/all_gather | solution.py:15
  165.9 1.5 copy-start.1
  182.7 27.3 %copy-start.3 = (s32[3]{0:T(128)S(1)}, s32[3]{0:T(128)}, u32[]{:S(2)}) copy-start(s32[3]{0:T(128)} %param.6) | copy-start | bytes 40
  182.7 928.5 %all-to-all-start.2 = ((bf16[32,4,384,104]{2,3,1,0:T(8,128)(2,1)}), bf16[32,4,384,104]{2,3,1,0:T(8,128)(2,1)}, u32[]{:S(2)}, u32[]{:S(2)}) async-start(bf16[32,4,384,104]{2,3,1,0:T(8,128)(2,1)} %stack.7), calls=%async_computation.2 | async-start | bytes 20447232 | tf_op jit(solution)/shard_map/all_to_all | solution.py:41
  1111.2 8.9 copy-start.2
Sparse Core Ops, SparseCore 0:
  96.3 53.1 all-gather.2
